TPU v7x, 32 devices: a whole 2x2x4 slice. The times are simulated.
32 devices in a mesh: ep: 4 (over y, x), edp: 4 (over z), tp: 2 (over core).
Axes of the slice: x: 2, y: 2, z: 4, core: 2. Of those that a mesh axis runs over, the one named last changes fastest.
Arguments:
- tokens: bfloat16 [2048, 4096], P(('ep', 'edp'), 'tp'), may hold values from -6 to 6
- cotangent: bfloat16 [2048, 4096], P(('ep', 'edp'), 'tp'), may hold values from -6 to 6
- expert_ids: int32 [2048, 8], P(('ep', 'edp')), may hold values from 0 to 127, all different within a row; in each aligned block of 128 rows (0 to 127, 128 to 255, ...) at most 10 rows name the same one
- route_weights: float32 [2048, 8], P(('ep', 'edp')), may hold values from 0.1 to 1
- expert_weights: bfloat16 [3, 1536, 4096], P(None, ('ep', 'tp')), may hold values from -0.15625 to 0.15625
Outputs:
- mixed: bfloat16 [2048, 4096], P(('ep', 'edp'), 'tp')
- grad_tokens: bfloat16 [2048, 4096], P(('ep', 'edp'), 'tp')
- weight_grads: float32 [3, 1536, 4096], P(None, ('ep', 'tp'), 'edp')
Inputs may be any that keep to these rules, and one draw needn't show every extreme that they name: `expert_ids`: each token names 8 different experts; within the tokens of one (ep, edp) index no expert is named by more than 10 tokens.
All inputs are finite; a program needn't handle non-finite values.
Results may differ from a plain program's by a relative error of at most 0.017.
Values may be sent and summed in bfloat16 or wider, within the bound.
A program may use at most 64 MiB of HBM per device.

v0:
```python
import jax
import jax.numpy as jnp
from jax import lax
from jax.sharding import PartitionSpec as P

CAP = 10


def route_tables(expert_ids, route_weights, window):
    tok_rows, top_count = expert_ids.shape
    flat_ids = expert_ids.reshape(-1)
    matches = (flat_ids[:, None] == jnp.arange(window, dtype=jnp.int32)[None, :]).astype(jnp.int32)
    slot_index = jnp.sum(matches * (jnp.cumsum(matches, axis=0) - 1), axis=1)
    in_slot = (slot_index[:, None] == jnp.arange(CAP, dtype=jnp.int32)[None, :]).astype(jnp.float32)
    placed = matches.astype(jnp.float32)[:, :, None] * in_slot[:, None, :]
    placed = placed.reshape(tok_rows, top_count, window, CAP)
    select = jnp.sum(placed, axis=1)
    weighted = jnp.sum(placed * route_weights[:, :, None, None], axis=1)
    return (select, weighted)


def pack_rows(select, weighted, features, grads_in):
    packed = jnp.einsum(
        "tec,td->ecd", select.astype(jnp.bfloat16), features, preferred_element_type=jnp.float32
    ).astype(jnp.bfloat16)
    scaled = jnp.einsum(
        "tec,td->ecd", weighted, grads_in.astype(jnp.float32), precision=lax.Precision.HIGHEST
    ).astype(jnp.bfloat16)
    return (jnp.repeat(packed, 4, axis=0), jnp.repeat(scaled, 4, axis=0))


def replica_sum(left, right):
    partial_sums = jnp.einsum("prs,prd->psd", left, right, preferred_element_type=jnp.float32)
    rounded = lax.optimization_barrier(partial_sums.astype(jnp.bfloat16)).astype(jnp.float32)
    return jnp.sum(rounded, axis=0)


def shards(tokens, cotangent, expert_ids, route_weights, expert_weights):
    n_devices = lax.axis_size("ep")
    window = n_devices // 4
    select, weighted = route_tables(expert_ids, route_weights, window)
    whole_tokens, whole_grads = (
        lax.all_gather(tokens, "tp", axis=1, tiled=True),
        lax.all_gather(cotangent, "tp", axis=1, tiled=True),
    )
    packed, scaled = pack_rows(select, weighted, whole_tokens, whole_grads)
    rows_in, grads_in = (
        lax.all_to_all(packed, "ep", split_axis=0, concat_axis=0, tiled=True),
        lax.all_to_all(scaled, "ep", split_axis=0, concat_axis=0, tiled=True),
    )
    width = rows_in.shape[2]
    token_rows = rows_in.reshape(-1, width)
    grad_rows = grads_in.reshape(-1, width)
    gate_up = jnp.einsum(
        "rd,jfd->jrf", token_rows, expert_weights[:2], preferred_element_type=jnp.float32
    )
    gate_val = gate_up[0]
    up_val = gate_up[1]
    gate_weight = expert_weights[0]
    up_weight = expert_weights[1]
    down_weight = expert_weights[2]
    sigmoid_gate = jax.nn.sigmoid(gate_val)
    active = gate_val * sigmoid_gate
    hidden = (active * up_val).astype(jnp.bfloat16)
    out_part = jnp.dot(hidden, down_weight, preferred_element_type=jnp.float32)
    contract_last = (((1,), (1,)), ((), ()))
    d_hidden = lax.dot_general(
        grad_rows, down_weight, contract_last, preferred_element_type=jnp.float32
    )
    d_gate = (d_hidden * up_val * sigmoid_gate * (1.0 + gate_val * (1.0 - sigmoid_gate))).astype(
        jnp.bfloat16
    )
    d_up = (d_hidden * active).astype(jnp.bfloat16)
    back_part = jnp.dot(d_gate, gate_weight, preferred_element_type=jnp.float32) + jnp.dot(
        d_up, up_weight, preferred_element_type=jnp.float32
    )
    replicas = lax.axis_size("edp")
    rows_block, grads_block = (
        lax.all_to_all(token_rows, "edp", split_axis=1, concat_axis=0, tiled=True),
        lax.all_to_all(grad_rows, "edp", split_axis=1, concat_axis=0, tiled=True),
    )
    left_factors = lax.all_gather(jnp.stack([d_gate, d_up, hidden]), "edp", axis=1, tiled=True)
    block_width = rows_block.shape[1]
    rows_block = rows_block.reshape(replicas, -1, block_width)
    grads_block = grads_block.reshape(replicas, -1, block_width)
    left_factors = left_factors.reshape(3, replicas, -1, left_factors.shape[2])
    weight_grads = jnp.stack(
        [
            replica_sum(left_factors[0], rows_block),
            replica_sum(left_factors[1], rows_block),
            replica_sum(left_factors[2], grads_block),
        ]
    )
    out_sum, back_sum = (
        lax.psum_scatter(
            out_part.astype(jnp.bfloat16), "tp", scatter_dimension=1, tiled=True
        ).astype(jnp.float32),
        lax.psum_scatter(
            back_part.astype(jnp.bfloat16), "tp", scatter_dimension=1, tiled=True
        ).astype(jnp.float32),
    )
    home_out, home_back = (
        lax.all_to_all(
            out_sum.astype(jnp.bfloat16).reshape(n_devices, CAP, -1),
            "ep",
            split_axis=0,
            concat_axis=0,
            tiled=True,
        ),
        lax.all_to_all(
            back_sum.astype(jnp.bfloat16).reshape(n_devices, CAP, -1),
            "ep",
            split_axis=0,
            concat_axis=0,
            tiled=True,
        ),
    )
    pair_out = home_out.astype(jnp.float32).reshape(window, 4, CAP, -1).sum(axis=1)
    pair_back = home_back.astype(jnp.float32).reshape(window, 4, CAP, -1).sum(axis=1)
    mixed = jnp.einsum("tec,ecd->td", weighted, pair_out, precision=lax.Precision.HIGHEST).astype(
        jnp.bfloat16
    )
    grad_tokens = jnp.einsum(
        "tec,ecd->td", select, pair_back, precision=lax.Precision.HIGHEST
    ).astype(jnp.bfloat16)
    return (mixed, grad_tokens, weight_grads)


def solution(mesh):
    placed = (
        P(("ep", "edp"), "tp"),
        P(("ep", "edp"), "tp"),
        P(("ep", "edp"), None),
        P(("ep", "edp"), None),
        P(None, ("ep", "tp"), None),
    )
    return jax.shard_map(
        shards,
        mesh=mesh,
        in_specs=placed,
        out_specs=(P(("ep", "edp"), "tp"), P(("ep", "edp"), "tp"), P(None, ("ep", "tp"), "edp")),
        check_vma=False,
    )
```

profile of v0, /device:TPU:0, one launch (start us, length us, event | category | flops | bytes accessed | tf_op | source)
XLA Modules:
  0.0 122.3 jit_solution(8222102204199329675)
XLA Ops:
  11.3 10.0 %all-gather.3.cloned.1.call-done = bf16[128,4096]{1,0:T(8,128)(2,1)} async-done(((bf16[128,2048]{1,0:T(8,128)(2,1)}), bf16[128,4096]{1,0:T(8,128)(2,1)}) %all-gather.3.cloned.1.call-update) | async-done | bytes 1048592 | tf_op jit(solution)/shard_map/all_gather | solution.py:43
  21.3 1.5 %convolution_convert_fusion.2 = bf16[10,4096]{1,0:T(8,128)(2,1)S(1)} fusion(bf16[128,4096]{1,0:T(8,128)(2,1)} %all-gather.3.cloned.1.call-done, f32[128,10]{0,1:T(8,128)S(1)} %get-tuple-element.3), kind=kOutput, calls=%fused_computation.4 | convolution fusion | flops 10528000 | bytes 1135616 | tf_op jit(solution)/shard_map/tec,td->ecd/dot_general | solution.py:23
  22.8 0.8 reshape.215
  23.6 3.9 %all-to-all-start = ((bf16[4,10,4096]{2,1,0:T(8,128)(2,1)}), bf16[4,10,4096]{2,1,0:T(8,128)(2,1)S(1)}, u32[]{:S(2)}, u32[]{:S(2)}) async-start(bf16[4,10,4096]{2,1,0:T(8,128)(2,1)} %reshape.215), calls=%async_computation | async-start | bytes 1048576 | tf_op jit(solution)/shard_map/all_to_all | solution.py:48
  27.6 5.5 %all-gather.5.cloned.1.call-done = bf16[128,4096]{1,0:T(8,128)(2,1)} async-done(((bf16[128,2048]{1,0:T(8,128)(2,1)}), bf16[128,4096]{1,0:T(8,128)(2,1)}) %all-gather.5.cloned.1.call-update) | async-done | bytes 1048592 | tf_op jit(solution)/shard_map/all_gather | solution.py:44
  33.1 1.7 %convolution_convert_fusion.1 = bf16[10,4096]{1,0:T(8,128)(2,1)S(1)} fusion(f32[128,10]{0,1:T(8,128)S(1)} %get-tuple-element.4, bf16[128,4096]{1,0:T(8,128)(2,1)} %all-gather.5.cloned.1.call-done), kind=kOutput, calls=%fused_computation.3 | convolution fusion | flops 62955520 | bytes 1135616 | tf_op jit(solution)/shard_map/tec,td->ecd/dot_general | solution.py:26
  34.9 1.2 all-to-all-done
  36.0 0.8 reshape.218
  36.9 3.5 %all-to-all-start.2 = ((bf16[4,10,4096]{2,1,0:T(8,128)(2,1)}), bf16[4,10,4096]{2,1,0:T(8,128)(2,1)S(1)}, u32[]{:S(2)}, u32[]{:S(2)}) async-start(bf16[4,10,4096]{2,1,0:T(8,128)(2,1)} %reshape.218), calls=%async_computation.3 | async-start | bytes 1048576 | tf_op jit(solution)/shard_map/all_to_all | solution.py:49
  40.5 3.0 %fusion.13 = f32[2,40,192]{2,1,0:T(8,128)S(1)} fusion(bf16[40,4096,1]{1,0,2:T(8,128)(2,1)S(1)} %reshape.222, bf16[3,192,4096]{2,1,0:T(8,128)(2,1)} %param.9), kind=kOutput, calls=%fused_computation.26 | convolution fusion | flops 125829120 | bytes 3534848 | tf_op jit(solution)/shard_map/rd,jfd->jrf/dot_general | solution.py:54
  43.5 4.6 %all-to-all-done.2 = bf16[4,10,4096]{2,1,0:T(8,128)(2,1)S(1)} async-done(((bf16[4,10,4096]{2,1,0:T(8,128)(2,1)}), bf16[4,10,4096]{2,1,0:T(8,128)(2,1)S(1)}, u32[]{:S(2)}, u32[]{:S(2)}) %all-to-all-start.2) | async-done | bytes 327712 | tf_op jit(solution)/shard_map/all_to_all | solution.py:49
  48.2 2.0 %fusion.27 = (bf16[40,192]{1,0:T(8,128)(2,1)S(1)}, bf16[40,192]{1,0:T(8,128)(2,1)S(1)}) fusion(f32[2,40,192]{2,1,0:T(8,128)S(1)} %fusion.13, bf16[40,4096]{1,0:T(8,128)(2,1)S(1)} %reshape.219, bf16[3,192,4096]{2,1,0:T(8,128)(2,1)} %param.9), kind=kOutput, calls=%fused_computation.46 | convolution fusion | flops 63014400 | bytes 1992704 | tf_op jit(solution)/shard_map/dot_general | solution.py:67
  50.2 1.8 %fusion.4 = f32[40,4096]{1,0:T(8,128)S(1)} fusion(bf16[40,192]{1,0:T(8,128)(2,1)S(1)} %get-tuple-element.11, bf16[3,192,4096]{2,1,0:T(8,128)(2,1)} %param.9), kind=kOutput, calls=%fused_computation.17 | convolution fusion | flops 62914560 | bytes 2243584 | tf_op jit(solution)/shard_map/dot_general | solution.py:74
  52.0 2.5 %fusion = bf16[40,4096]{1,0:T(8,128)(2,1)} fusion(f32[40,4096]{1,0:T(8,128)S(1)} %fusion.4, bf16[40,192]{1,0:T(8,128)(2,1)S(1)} %get-tuple-element.10, bf16[3,192,4096]{2,1,0:T(8,128)(2,1)} %param.9), kind=kOutput, calls=%fused_computation.1 | convolution fusion | flops 63242240 | bytes 2571264 | tf_op jit(solution)/shard_map/dot_general | solution.py:74
  55.6 4.7 %all-to-all-start.4 = ((bf16[40,4,1024]{2,0,1:T(8,128)(2,1)}), bf16[40,4,1024]{2,0,1:T(8,128)(2,1)S(1)}, u32[]{:S(2)}, u32[]{:S(2)}) async-start(bf16[40,4,1024]{2,0,1:T(8,128)(2,1)} %copy.30), calls=%async_computation.6 | async-start | bytes 655360 | tf_op jit(solution)/shard_map/all_to_all | solution.py:79
  60.3 2.5 %convolution_convert_fusion = bf16[40,4096]{1,0:T(8,128)(2,1)} fusion(bf16[3,192,4096]{2,1,0:T(8,128)(2,1)} %param.9, bf16[1,40,192]{2,1,0:T(8,128)(2,1)S(1)} %multiply_convert_fusion), kind=kOutput, calls=%fused_computation.2 | convolution fusion | flops 63078400 | bytes 1915904 | tf_op jit(solution)/shard_map/dot_general | solution.py:65
  63.1 0.8 copy.31
  64.0 14.8 %all_gather.11 = bf16[3,160,192]{2,1,0:T(8,128)(2,1)S(1)} all-gather(bf16[3,40,192]{2,1,0:T(8,128)(2,1)S(1)} %pad_maximum_fusion.1), channel_id=1, replica_groups=mesh['ep'=4,'edp'=4,'tp'=2] {'edp'}, dimensions={1}, use_global_device_ids=true | all-gather | bytes 230400 | tf_op jit(solution)/shard_map/all_gather | solution.py:82
  79.5 4.1 %all-to-all-start.5 = ((bf16[40,4,1024]{2,0,1:T(8,128)(2,1)}), bf16[40,4,1024]{2,0,1:T(8,128)(2,1)}, u32[]{:S(2)}, u32[]{:S(2)}) async-start(bf16[40,4,1024]{2,0,1:T(8,128)(2,1)} %copy.31), calls=%async_computation.7 | async-start | bytes 655360 | tf_op jit(solution)/shard_map/all_to_all | solution.py:80
  84.2 1.5 %convolution_convert_fusion.6 = bf16[4,192,1024]{2,1,0:T(8,128)(2,1)S(1)} fusion(bf16[4,40,192]{2,1,0:T(8,128)(2,1)} %bitcast.87, bf16[40,4,1024]{2,0,1:T(8,128)(2,1)S(1)} %all-to-all-done.4), kind=kOutput, calls=%fused_computation.14 | convolution fusion | flops 63700992 | bytes 1961984 | tf_op jit(solution)/shard_map/prs,prd->psd/dot_general | solution.py:33
  85.7 5.3 %all-to-all-done.5 = bf16[40,4,1024]{2,0,1:T(8,128)(2,1)} async-done(((bf16[40,4,1024]{2,0,1:T(8,128)(2,1)}), bf16[40,4,1024]{2,0,1:T(8,128)(2,1)}, u32[]{:S(2)}, u32[]{:S(2)}) %all-to-all-start.5) | async-done | bytes 327712 | tf_op jit(solution)/shard_map/all_to_all | solution.py:80
  91.0 1.6 %convolution_convert_fusion.5 = bf16[4,192,1024]{2,1,0:T(8,128)(2,1)S(1)} fusion(bf16[4,40,192]{2,1,0:T(8,128)(2,1)S(1)} %bitcast.86, bf16[40,4,1024]{2,0,1:T(8,128)(2,1)} %all-to-all-done.5), kind=kOutput, calls=%fused_computation.13 | convolution fusion | flops 63700992 | bytes 1961984 | tf_op jit(solution)/shard_map/prs,prd->psd/dot_general | solution.py:33
  92.6 1.2 convert_reduce_fusion.2
  94.3 1.7 %reshape.220 = bf16[4,10,2048]{2,1,0:T(8,128)(2,1)} reshape(bf16[40,2048]{1,0:T(8,128)(2,1)} %reduce-scatter.5.cloned.1.call-done) | data formatting | bytes 327680 | tf_op jit(solution)/shard_map/reshape | solution.py:111
  96.0 3.4 %all-to-all-start.3 = ((bf16[4,10,2048]{2,1,0:T(8,128)(2,1)}), bf16[4,10,2048]{2,1,0:T(8,128)(2,1)S(1)}, u32[]{:S(2)}, u32[]{:S(2)}) async-start(bf16[4,10,2048]{2,1,0:T(8,128)(2,1)} %reshape.220), calls=%async_computation.5 | async-start | bytes 524288 | tf_op jit(solution)/shard_map/all_to_all | solution.py:110
  99.4 1.6 %pad_maximum_fusion = f32[3,192,1024]{2,1,0:T(8,128)} fusion(f32[1,192,1024]{2,1,0:T(8,128)S(1)} %bitcast.85, f32[1,192,1024]{2,1,0:T(8,128)S(1)} %bitcast.84, f32[1,192,1024]{2,1,0:T(8,128)S(1)} %bitcast.83), kind=kLoop, calls=%fused_computation.12 | loop fusion | flops 1179648 | bytes 4718592 | tf_op jit(solution)/shard_map/stack | solution.py:87
  101.0 1.7 %reshape.217 = bf16[4,10,2048]{2,1,0:T(8,128)(2,1)} reshape(bf16[40,2048]{1,0:T(8,128)(2,1)} %reduce-scatter.3.cloned.1.call-done) | data formatting | bytes 327680 | tf_op jit(solution)/shard_map/reshape | solution.py:104
  102.7 2.4 %all-to-all-done.3 = bf16[4,10,2048]{2,1,0:T(8,128)(2,1)S(1)} async-done(((bf16[4,10,2048]{2,1,0:T(8,128)(2,1)}), bf16[4,10,2048]{2,1,0:T(8,128)(2,1)S(1)}, u32[]{:S(2)}, u32[]{:S(2)}) %all-to-all-start.3) | async-done | bytes 163872 | tf_op jit(solution)/shard_map/all_to_all | solution.py:110
  105.1 3.4 %all-to-all-start.1 = ((bf16[4,10,2048]{2,1,0:T(8,128)(2,1)}), bf16[4,10,2048]{2,1,0:T(8,128)(2,1)S(1)}, u32[]{:S(2)}, u32[]{:S(2)}) async-start(bf16[4,10,2048]{2,1,0:T(8,128)(2,1)} %reshape.217), calls=%async_computation.2 | async-start | bytes 524288 | tf_op jit(solution)/shard_map/all_to_all | solution.py:103
  108.6 1.8 %convolution_convert_fusion.3 = bf16[128,2048]{1,0:T(8,128)(2,1)} fusion(f32[128,10]{0,1:T(8,128)S(1)} %copy-done.4, f32[10,2048]{1,0:T(8,128)S(1)} %convert_reduce_fusion.3), kind=kOutput, calls=%fused_computation.10 | convolution fusion | flops 31719424 | bytes 611328 | tf_op jit(solution)/shard_map/tec,ecd->td/dot_general | solution.py:123
  110.4 3.5 %all-to-all-done.1 = bf16[4,10,2048]{2,1,0:T(8,128)(2,1)S(1)} async-done(((bf16[4,10,2048]{2,1,0:T(8,128)(2,1)}), bf16[4,10,2048]{2,1,0:T(8,128)(2,1)S(1)}, u32[]{:S(2)}, u32[]{:S(2)}) %all-to-all-start.1) | async-done | bytes 163872 | tf_op jit(solution)/shard_map/all_to_all | solution.py:103
  113.9 1.8 %convolution_convert_fusion.4 = bf16[128,2048]{1,0:T(8,128)(2,1)} fusion(f32[128,10]{0,1:T(8,128)S(1)} %copy-done.2, f32[10,2048]{1,0:T(8,128)S(1)} %convert_reduce_fusion.4), kind=kOutput, calls=%fused_computation.11 | convolution fusion | flops 31719424 | bytes 611328 | tf_op jit(solution)/shard_map/tec,ecd->td/dot_general | solution.py:120
  (49 shorter events, 7.6 us)
Async XLA Ops:
  7.2 14.2 %all-gather.3.cloned.1.call-start = ((), (), s32[]{:S(2)}) async-start(), calls=%async_computation.8 | async-start | bytes 1572864 | tf_op jit(solution)/shard_map/all_gather | solution.py:43
  7.9 25.2 %all-gather.5.cloned.1.call-start = ((), (), s32[]{:S(2)}) async-start(), calls=%async_computation.10 | async-start | bytes 1572864 | tf_op jit(solution)/shard_map/all_gather | solution.py:44
  11.3 12.3 %copy-start.3 = (f32[128,10]{0,1:T(8,128)}, f32[128,10]{0,1:T(8,128)S(1)}, u32[]{:S(2)}) copy-start(f32[128,10]{0,1:T(8,128)S(1)} %get-tuple-element.3) | copy-start | bytes 15364
  11.3 25.5 %copy-start.1 = (f32[128,10]{0,1:T(8,128)}, f32[128,10]{0,1:T(8,128)S(1)}, u32[]{:S(2)}) copy-start(f32[128,10]{0,1:T(8,128)S(1)} %get-tuple-element.4) | copy-start | bytes 15364
  23.6 12.4 %all-to-all-start = ((bf16[4,10,4096]{2,1,0:T(8,128)(2,1)}), bf16[4,10,4096]{2,1,0:T(8,128)(2,1)S(1)}, u32[]{:S(2)}, u32[]{:S(2)}) async-start(bf16[4,10,4096]{2,1,0:T(8,128)(2,1)} %reshape.215), calls=%async_computation | async-start | bytes 1048576 | tf_op jit(solution)/shard_map/all_to_all | solution.py:48
  36.9 11.2 %all-to-all-start.2 = ((bf16[4,10,4096]{2,1,0:T(8,128)(2,1)}), bf16[4,10,4096]{2,1,0:T(8,128)(2,1)S(1)}, u32[]{:S(2)}, u32[]{:S(2)}) async-start(bf16[4,10,4096]{2,1,0:T(8,128)(2,1)} %reshape.218), calls=%async_computation.3 | async-start | bytes 1048576 | tf_op jit(solution)/shard_map/all_to_all | solution.py:49
  40.3 54.0 %reduce-scatter.5.cloned.1.call-start = ((), (), s32[]{:S(2)}) async-start(), calls=%async_computation.11 | async-start | bytes 491520 | tf_op jit(solution)/shard_map/reduce_scatter | solution.py:98
  55.6 23.8 %all-to-all-start.4 = ((bf16[40,4,1024]{2,0,1:T(8,128)(2,1)}), bf16[40,4,1024]{2,0,1:T(8,128)(2,1)S(1)}, u32[]{:S(2)}, u32[]{:S(2)}) async-start(bf16[40,4,1024]{2,0,1:T(8,128)(2,1)} %copy.30), calls=%async_computation.6 | async-start | bytes 655360 | tf_op jit(solution)/shard_map/all_to_all | solution.py:79
  60.3 40.7 %reduce-scatter.3.cloned.1.call-start = ((), (), s32[]{:S(2)}) async-start(), calls=%async_computation.9 | async-start | bytes 491520 | tf_op jit(solution)/shard_map/reduce_scatter | solution.py:95
  79.5 11.5 %all-to-all-start.5 = ((bf16[40,4,1024]{2,0,1:T(8,128)(2,1)}), bf16[40,4,1024]{2,0,1:T(8,128)(2,1)}, u32[]{:S(2)}, u32[]{:S(2)}) async-start(bf16[40,4,1024]{2,0,1:T(8,128)(2,1)} %copy.31), calls=%async_computation.7 | async-start | bytes 655360 | tf_op jit(solution)/shard_map/all_to_all | solution.py:80
  93.7 5.7 %copy-start = (f32[192,1024]{1,0:T(8,128)S(1)}, f32[192,1024]{1,0:T(8,128)}, u32[]{:S(2)}) copy-start(f32[192,1024]{1,0:T(8,128)} %convert_reduce_fusion.2) | copy-start | bytes 2359300
  96.0 9.1 %all-to-all-start.3 = ((bf16[4,10,2048]{2,1,0:T(8,128)(2,1)}), bf16[4,10,2048]{2,1,0:T(8,128)(2,1)S(1)}, u32[]{:S(2)}, u32[]{:S(2)}) async-start(bf16[4,10,2048]{2,1,0:T(8,128)(2,1)} %reshape.220), calls=%async_computation.5 | async-start | bytes 524288 | tf_op jit(solution)/shard_map/all_to_all | solution.py:110
  99.4 9.1 %copy-start.4 = (f32[128,10]{0,1:T(8,128)S(1)}, f32[128,10]{0,1:T(8,128)}, u32[]{:S(2)}) copy-start(f32[128,10]{0,1:T(8,128)} %copy-done.3) | copy-start | bytes 15364
  101.0 12.9 %copy-start.2 = (f32[128,10]{0,1:T(8,128)S(1)}, f32[128,10]{0,1:T(8,128)}, u32[]{:S(2)}) copy-start(f32[128,10]{0,1:T(8,128)} %copy-done.1) | copy-start | bytes 15364
  105.1 8.8 %all-to-all-start.1 = ((bf16[4,10,2048]{2,1,0:T(8,128)(2,1)}), bf16[4,10,2048]{2,1,0:T(8,128)(2,1)S(1)}, u32[]{:S(2)}, u32[]{:S(2)}) async-start(bf16[4,10,2048]{2,1,0:T(8,128)(2,1)} %reshape.217), calls=%async_computation.2 | async-start | bytes 524288 | tf_op jit(solution)/shard_map/all_to_all | solution.py:103
Sparse Core Ops, SparseCore 0:
  9.5 11.7 all-gather.2
  22.9 10.1 all-gather.4
  54.7 7.8 reduce-scatter.4
  65.3 8.8 reduce-scatter.2
where the time goes:
time: 123 us; the launch traced here: 122 us
  waiting for transfers between devices  33.9 us (28%)
  starting transfers between devices  23.1 us (19%)
  matrix products  22.4 us (18%)
  blocking collectives  14.8 us (12%)
  between operations  14 us (11%)
  local copies, waits for them, and re-layouts  8.74 us (7%)
  other arithmetic  5.3 us (4%)
    all_gather x1, blocking collectives, shards(): lax.all_gather(jnp.stack([d_gate, d_up, hidden]), 'edp', axis=1, tiled=True)  14.8 us
    all_gather x1, waiting for transfers between devices, shards(): lax.all_gather(tokens, 'tp', axis=1, tiled=True)  10 us
    all_gather x1, waiting for transfers between devices, shards(): lax.all_gather(cotangent, 'tp', axis=1, tiled=True)  5.55 us
    all_to_all x1, waiting for transfers between devices, shards(): lax.all_to_all(grad_rows, 'edp', split_axis=1, concat_axis=0, tiled=True)  5.29 us
    all_to_all x1, starting transfers between devices, shards(): lax.all_to_all(token_rows, 'edp', split_axis=1, concat_axis=0, tiled=True)  4.67 us
    all_to_all x1, waiting for transfers between devices, shards(): lax.all_to_all(scaled, 'ep', split_axis=0, concat_axis=0, tiled=True)  4.58 us
    all_to_all x1, starting transfers between devices, shards(): lax.all_to_all(grad_rows, 'edp', split_axis=1, concat_axis=0, tiled=True)  4.11 us
    all_to_all x1, starting transfers between devices, shards(): lax.all_to_all(packed, 'ep', split_axis=0, concat_axis=0, tiled=True)  3.92 us
  transfers between devices with their start and end apart: 10, of which 7 were waited for; matrix products, arithmetic and copies ran while one was open for 22% of the time, Pallas kernels for 0%

commit v1 on v0

v1 whole, which is shorter than its diff:
```python
import functools

import jax
import jax.numpy as jnp
import numpy as np
from jax import lax
from jax.experimental import pallas as pl
from jax.experimental.pallas import tpu as pltpu
from jax.sharding import PartitionSpec as P

CAP = 10
PARTS = 4
MESH = pl.DeviceIdType.MESH
F32 = jnp.float32
BF16 = jnp.bfloat16


def round_up(value, unit):
    return -(-value // unit) * unit


class Sizes:
    def __init__(self, ep, edp, tp, tok_rows, feats, hid):
        self.ep, self.edp, self.tp = ep, edp, tp
        self.window = ep // PARTS
        self.tok_rows, self.feats, self.hid = tok_rows, feats, hid
        self.block = feats * tp // edp
        self.nblk = feats // self.block
        self.nch = max(1, min(4, self.block // 128))
        self.cw = self.block // self.nch
        self.xr = round_up(2 * CAP * self.nch, 16)
        self.rows = round_up(ep * CAP, 16)


def permutation(z):
    table = np.zeros((z.nch, 2, z.rows, z.ep, z.xr), np.float32)
    for q in range(z.nch):
        for a in range(2):
            for i in range(z.ep):
                for c in range(CAP):
                    table[q, a, i * CAP + c, i, (2 * q + a) * CAP + c] = 1.0
    flat = table.reshape(z.nch, 2 * z.rows, z.ep * z.xr)
    return flat.reshape(-1, z.ep * z.xr), np.swapaxes(flat, 1, 2).copy()


def slot_parts(index, nch):
    chunk = jnp.zeros_like(index)
    for k in range(1, nch):
        chunk += (index >= 2 * CAP * k).astype(jnp.int32)
    rest = index - 2 * CAP * chunk
    array = (rest >= CAP).astype(jnp.int32)
    return chunk, array, rest - CAP * array


def kernel(
    z, tok, cot, ids, rw, perm, perm_t, weights,
    mixed, grad_tok, wgrad,
    wb, x, xin, rb, rows, pout, pin, hb, lb, ob, y, yin, right,
    w_loc, w_send, w_recv, x_send, x_recv, r_send, r_recv, p_send, p_recv,
    l_send, l_recv, y_send, y_recv, q_send, q_recv,
):
    i, e, s = lax.axis_index("ep"), lax.axis_index("edp"), lax.axis_index("tp")
    barrier = pltpu.get_barrier_semaphore()
    group = z.ep * z.edp

    def greet(step, carry):
        di = step // z.edp
        de = step - di * z.edp
        pl.semaphore_signal(
            barrier, inc=1,
            device_id=(lax.rem(i + di, z.ep), lax.rem(e + de, z.edp), s),
            device_id_type=MESH,
        )
        return carry

    for d in range(1, z.tp):
        pl.semaphore_signal(
            barrier, inc=1, device_id=(i, e, lax.rem(s + d, z.tp)), device_id_type=MESH
        )
    lax.fori_loop(1, group, greet, 0)

    own_w = pltpu.make_async_copy(
        weights.at[:, :, pl.ds(pl.multiple_of(s * z.feats, 128), z.feats)], wb.at[s], w_loc
    )
    own_w.start()

    ids_t = jnp.transpose(ids[...].astype(F32))
    rw_t = jnp.transpose(rw[...])
    top = ids_t.shape[0]
    row = lax.broadcasted_iota(jnp.int32, (z.xr, z.tok_rows), 0)
    chunk, array, slot = slot_parts(row, z.nch)
    in_use = row < 2 * CAP * z.nch
    before = (
        lax.broadcasted_iota(jnp.int32, (z.tok_rows, z.tok_rows), 0)
        < lax.broadcasted_iota(jnp.int32, (z.tok_rows, z.tok_rows), 1)
    ).astype(F32).astype(BF16)
    picks, scales = [], []
    for w in range(z.window):
        hit = (ids_t == float(w)).astype(F32)
        match = jnp.sum(hit, axis=0, keepdims=True)
        weight = jnp.sum(hit * rw_t, axis=0, keepdims=True)
        match_all = jnp.broadcast_to(match, (z.xr, z.tok_rows))
        rank = jnp.dot(match_all.astype(BF16), before, preferred_element_type=F32)
        pick = jnp.where(in_use & (rank == slot.astype(F32)), match_all, 0.0)
        slot_weight = jnp.sum(pick * weight, axis=1, keepdims=True)
        scale = jnp.where(array[:, :1] == 1, slot_weight, 1.0)
        picks.append(pick)
        scales.append(jnp.where(array[:, :1] == 0, slot_weight, 1.0))
        for b in range(z.nblk):
            total = jnp.zeros((z.xr, z.cw), F32)
            for q in range(z.nch):
                cols = pl.ds(b * z.block + q * z.cw, z.cw)
                for a, source in ((0, tok), (1, cot)):
                    chosen = jnp.where((chunk == q) & (array == a), pick, 0.0).astype(BF16)
                    total += jnp.dot(chosen, source[:, cols], preferred_element_type=F32)
            x[w, b] = (total * scale).astype(BF16)

    pl.semaphore_wait(barrier, group - 1 + z.tp - 1)

    w_copies = []
    for d in range(1, z.tp):
        to = lax.rem(s + d, z.tp)
        w_copies.append(pltpu.make_async_remote_copy(
            src_ref=weights.at[:, :, pl.ds(pl.multiple_of(to * z.feats, 128), z.feats)],
            dst_ref=wb.at[s], send_sem=w_send.at[d], recv_sem=w_recv.at[s],
            device_id=(i, e, to), device_id_type=MESH,
        ))
    x_copies = []
    for d in range(1, z.ep):
        to = lax.rem(i + d, z.ep)
        x_copies.append(pltpu.make_async_remote_copy(
            src_ref=x.at[to // PARTS], dst_ref=xin.at[i],
            send_sem=x_send.at[d], recv_sem=x_recv.at[i],
            device_id=(to, e, s), device_id_type=MESH,
        ))
    for copy in x_copies + w_copies:
        copy.start()

    def right_copy(b, d):
        to = lax.rem(i + d, z.ep)
        return pltpu.make_async_remote_copy(
            src_ref=x.at[to // PARTS, b], dst_ref=rb.at[e, i],
            send_sem=r_send.at[b * z.ep + d], recv_sem=r_recv.at[0],
            device_id=(to, s * z.nblk + b, s), device_id_type=MESH,
        )

    for b in range(z.nblk):
        @pl.when(s * z.nblk + b != e)
        def _():
            for d in range(z.ep):
                right_copy(b, d).start()

    xin[i] = x[i // PARTS]
    for d in range(1, z.ep):
        source = lax.rem(i + d, z.ep)
        pltpu.make_async_copy(xin.at[source], xin.at[source], x_recv.at[source]).wait()

    arrange = perm[...]

    def unpack(packed):
        return jnp.dot(arrange, packed, preferred_element_type=F32).astype(BF16)

    for b in range(z.nblk):
        flat = unpack(xin[:, b].reshape(z.ep * z.xr, z.cw))
        for q in range(z.nch):
            cols = pl.ds(b * z.block + q * z.cw, z.cw)
            rows[:, cols] = flat[q * 2 * z.rows:(q + 1) * 2 * z.rows]

    own_w.wait()
    for d in range(1, z.tp):
        source = lax.rem(s + d, z.tp)
        pltpu.make_async_copy(wb.at[source], wb.at[source], w_recv.at[source]).wait()

    last = (((1,), (1,)), ((), ()))
    for t in range(z.tp):
        for m in range(3):
            part = rows[:z.rows] if m < 2 else rows[z.rows:]
            pout[t, m] = lax.dot_general(part, wb[t, m], last, preferred_element_type=F32)
    p_copies = []
    for d in range(1, z.tp):
        to = lax.rem(s + d, z.tp)
        copy = pltpu.make_async_remote_copy(
            src_ref=pout, dst_ref=pin.at[s], send_sem=p_send.at[d], recv_sem=p_recv.at[s],
            device_id=(i, e, to), device_id_type=MESH,
        )
        copy.start()
        p_copies.append(copy)
    for d in range(1, z.tp):
        source = lax.rem(s + d, z.tp)
        pltpu.make_async_copy(pin.at[source], pin.at[source], p_recv.at[source]).wait()

    for t in range(z.tp):
        sums = []
        for m in range(3):
            value = pout[t, m]
            for d in range(1, z.tp):
                value += pin[lax.rem(s + d, z.tp), t, m]
            sums.append(value)
        gate, up, d_hidden = sums
        sig = jax.nn.sigmoid(gate)
        active = gate * sig
        hb[t, 0] = (d_hidden * up * sig * (1.0 + gate * (1.0 - sig))).astype(BF16)
        hb[t, 1] = (d_hidden * active).astype(BF16)
        hb[t, 2] = (active * up).astype(BF16)

    l_copies = []
    for d in range(1, z.edp):
        copy = pltpu.make_async_remote_copy(
            src_ref=hb.at[s], dst_ref=lb.at[e], send_sem=l_send.at[d], recv_sem=l_recv.at[e],
            device_id=(i, lax.rem(e + d, z.edp), s), device_id_type=MESH,
        )
        copy.start()
        l_copies.append(copy)
    lb[e] = hb[s]

    out = jnp.zeros((z.rows, z.feats), F32)
    back = jnp.zeros((z.rows, z.feats), F32)
    for t in range(z.tp):
        out += jnp.dot(hb[t, 2], wb[t, 2], preferred_element_type=F32)
        back += jnp.dot(hb[t, 0], wb[t, 0], preferred_element_type=F32)
        back += jnp.dot(hb[t, 1], wb[t, 1], preferred_element_type=F32)
    ob[:z.rows] = out.astype(BF16)
    ob[z.rows:] = back.astype(BF16)
    for b in range(z.nblk):
        total = jnp.zeros((z.ep * z.xr, z.cw), F32)
        for q in range(z.nch):
            cols = pl.ds(b * z.block + q * z.cw, z.cw)
            total += jnp.dot(perm_t[q], ob[:, cols], preferred_element_type=F32)
        y[:, b] = total.astype(BF16).reshape(z.ep, z.xr, z.cw)
    y_copies = []
    for d in range(1, z.ep):
        to = lax.rem(i + d, z.ep)
        copy = pltpu.make_async_remote_copy(
            src_ref=y.at[to], dst_ref=yin.at[i], send_sem=y_send.at[d], recv_sem=y_recv.at[i],
            device_id=(to, e, s), device_id_type=MESH,
        )
        copy.start()
        y_copies.append(copy)
    yin[i] = y[i]

    owner = e // z.nblk
    mine = e - owner * z.nblk

    def relay(d):
        return pltpu.make_async_remote_copy(
            src_ref=rb, dst_ref=rb, send_sem=q_send.at[d], recv_sem=q_recv.at[0],
            device_id=(i, e, lax.rem(s + d, z.tp)), device_id_type=MESH,
        )

    @pl.when(s == owner)
    def _():
        for source in range(z.ep):
            rb[e, source] = xin[source, mine]
        others = rb.at[pl.ds(0, z.edp - 1)]
        pltpu.make_async_copy(others, others, r_recv.at[0]).wait()
        for d in range(1, z.tp):
            relay(d).start()

    @pl.when(s != owner)
    def _():
        pltpu.make_async_copy(rb, rb, q_recv.at[0]).wait()

    for r in range(z.edp):
        flat = unpack(rb[r].reshape(z.ep * z.xr, z.cw))
        for q in range(z.nch):
            for a in range(2):
                at = (2 * q + a) * z.rows
                right[a, pl.ds(r * z.rows, z.rows), pl.ds(q * z.cw, z.cw)] = flat[at:at + z.rows]

    for d in range(1, z.ep):
        source = lax.rem(i + d, z.ep)
        pltpu.make_async_copy(yin.at[source], yin.at[source], y_recv.at[source]).wait()

    lane = lax.broadcasted_iota(jnp.int32, (z.tok_rows, z.xr), 1)
    lane_chunk, lane_array, _ = slot_parts(lane, z.nch)
    homes = [jnp.transpose(pick) for pick in picks]
    for b in range(z.nblk):
        sums = []
        for w in range(z.window):
            total = yin[w * PARTS, b].astype(F32)
            for h in range(1, PARTS):
                total += yin[w * PARTS + h, b].astype(F32)
            sums.append((total * scales[w]).astype(BF16))
        for q in range(z.nch):
            cols = pl.ds(b * z.block + q * z.cw, z.cw)
            for a, target in ((0, mixed), (1, grad_tok)):
                value = jnp.zeros((z.tok_rows, z.cw), F32)
                for w in range(z.window):
                    chosen = jnp.where((lane_chunk == q) & (lane_array == a), homes[w], 0.0).astype(BF16)
                    value += jnp.dot(chosen, sums[w], preferred_element_type=F32)
                target[:, cols] = value.astype(BF16)

    for d in range(1, z.edp):
        source = lax.rem(e + d, z.edp)
        pltpu.make_async_copy(lb.at[source], lb.at[source], l_recv.at[source]).wait()
    first = (((0,), (0,)), ((), ()))
    for m in range(3):
        left = lb[:, m].reshape(z.edp * z.rows, z.hid)
        wgrad[m] = lax.dot_general(left, right[1 if m == 2 else 0], first, preferred_element_type=F32)

    for copy in x_copies + w_copies + p_copies + l_copies + y_copies:
        copy.wait_send()
    for b in range(z.nblk):
        @pl.when(s * z.nblk + b != e)
        def _():
            for d in range(z.ep):
                right_copy(b, d).wait_send()

    @pl.when(s == owner)
    def _():
        for d in range(1, z.tp):
            relay(d).wait_send()


def shards(tokens, cotangent, expert_ids, route_weights, expert_weights):
    z = Sizes(
        lax.axis_size("ep"), lax.axis_size("edp"), lax.axis_size("tp"),
        tokens.shape[0], tokens.shape[1], expert_weights.shape[1],
    )
    perm, perm_t = permutation(z)
    vmem = pl.BlockSpec(memory_space=pltpu.VMEM)
    dma = pltpu.SemaphoreType.DMA
    return pl.pallas_call(
        functools.partial(kernel, z),
        out_shape=(
            jax.ShapeDtypeStruct(tokens.shape, BF16),
            jax.ShapeDtypeStruct(tokens.shape, BF16),
            jax.ShapeDtypeStruct((3, z.hid, z.block), F32),
        ),
        in_specs=[vmem] * 6 + [pl.BlockSpec(memory_space=pltpu.HBM)],
        out_specs=(vmem,) * 3,
        scratch_shapes=[
            pltpu.VMEM((z.tp, 3, z.hid, z.feats), BF16),
            pltpu.VMEM((z.window, z.nblk, z.xr, z.cw), BF16),
            pltpu.VMEM((z.ep, z.nblk, z.xr, z.cw), BF16),
            pltpu.VMEM((z.edp, z.ep, z.xr, z.cw), BF16),
            pltpu.VMEM((2 * z.rows, z.feats), BF16),
            pltpu.VMEM((z.tp, 3, z.rows, z.hid), F32),
            pltpu.VMEM((z.tp, z.tp, 3, z.rows, z.hid), F32),
            pltpu.VMEM((z.tp, 3, z.rows, z.hid), BF16),
            pltpu.VMEM((z.edp, 3, z.rows, z.hid), BF16),
            pltpu.VMEM((2 * z.rows, z.feats), BF16),
            pltpu.VMEM((z.ep, z.nblk, z.xr, z.cw), BF16),
            pltpu.VMEM((z.ep, z.nblk, z.xr, z.cw), BF16),
            pltpu.VMEM((2, z.edp * z.rows, z.block), BF16),
            dma, dma((z.tp,)), dma((z.tp,)), dma((z.ep,)), dma((z.ep,)),
            dma((z.nblk * z.ep,)), dma((1,)), dma((z.tp,)), dma((z.tp,)),
            dma((z.edp,)), dma((z.edp,)), dma((z.ep,)), dma((z.ep,)),
            dma((z.tp,)), dma((1,)),
        ],
        compiler_params=pltpu.CompilerParams(
            collective_id=0, has_side_effects=True, vmem_limit_bytes=60 * 1024 * 1024
        ),
        name="expert_block",
    )(
        tokens, cotangent, expert_ids, route_weights,
        jnp.asarray(perm, BF16), jnp.asarray(perm_t, BF16), expert_weights,
    )


def solution(mesh):
    placed = (
        P(("ep", "edp"), "tp"),
        P(("ep", "edp"), "tp"),
        P(("ep", "edp"), None),
        P(("ep", "edp"), None),
        P(None, ("ep", "tp"), None),
    )
    return jax.shard_map(
        shards,
        mesh=mesh,
        in_specs=placed,
        out_specs=(P(("ep", "edp"), "tp"), P(("ep", "edp"), "tp"), P(None, ("ep", "tp"), "edp")),
        check_vma=False,
    )
```

time: 123 us -> 39.3 us (0.32)
  waiting for transfers between devices: 33.9 us -> 0 us
  Pallas kernels: 0 us -> 28.4 us
  starting transfers between devices: 23.1 us -> 0 us
  matrix products: 22.4 us -> 0 us
  blocking collectives: 14.8 us -> 0 us
  between operations: 14 us -> 0.64 us
  other arithmetic: 5.3 us -> 0 us
    pallas_call x0 -> x1, Pallas kernels: none -> 28.4 us  [shards(): pl.pallas_call(functools.partial(kernel, z), out_shape=(jax.ShapeDtypeStr...]
    all_to_all x6 -> x0, starting transfers between devices: 23 us -> none  [the longest x1 4.67 us: shards(): lax.all_to_all(token_rows, 'edp', split_axis=1, concat_axis=0, tiled=True)]
    dot_general x12 -> x0, matrix products: 22.4 us -> none  [the longest x3 3.69 us: replica_sum(): jnp.einsum('prs,prd->psd', left, right, preferred_element_type=jnp.float32)]
    all_to_all x6 -> x0, waiting for transfers between devices: 16.9 us -> none  [the longest x1 5.29 us: shards(): lax.all_to_all(grad_rows, 'edp', split_axis=1, concat_axis=0, tiled=True)]
    all_gather x2 -> x0, waiting for transfers between devices: 15.5 us -> none  [the longest x1 10 us: shards(): lax.all_gather(tokens, 'tp', axis=1, tiled=True)]
    all_gather x1 -> x0, blocking collectives: 14.8 us -> none  [shards(): lax.all_gather(jnp.stack([d_gate, d_up, hidden]), 'edp', axis=1, tiled=True)]
    unnamed x10 -> x5, local copies, waits for them, and re-layouts: 0.02 us -> 9.95 us
    reshape x6 -> x0, local copies, waits for them, and re-layouts: 5.25 us -> none  [the longest x1 1.69 us: shards(): out_sum.astype(jnp.bfloat16).reshape(n_devices, CAP, -1)]
  transfers between devices with their start and end apart: 10 -> 0, of which waited for: 7 -> 0; matrix products, arithmetic and copies ran while one was open for 22% -> 0% of each run, Pallas kernels for 0% -> 0%
where the time goes in v1:
time: 39.3 us; the launch traced here: 38.9 us
  Pallas kernels  28.4 us (72%)
  local copies, waits for them, and re-layouts  9.95 us (25%)
  between operations  0.64 us (2%)
    pallas_call x1, Pallas kernels, shards(): pl.pallas_call(functools.partial(kernel, z), out_shape=(jax.ShapeDtypeStr...  28.4 us
    unnamed x5, local copies, waits for them, and re-layouts  9.95 us

profile of v1, /device:TPU:0, one launch (start us, length us, event | category | flops | bytes accessed | tf_op | source)
XLA Modules:
  0.0 38.9 jit_solution(15124298176035717179)
XLA Ops:
  0.6 1.4 %copy.10.ids = s32[128,8]{1,0:T(8,128)} copy(s32[128,8]{0,1:T(8,128)} %param.9) | data formatting | bytes 8192 | tf_op args[2]
  2.0 1.4 %copy.11.rw = f32[128,8]{1,0:T(8,128)} copy(f32[128,8]{0,1:T(8,128)} %param.10) | data formatting | bytes 8192 | tf_op args[3]
  3.5 28.4 %expert_block.1 = (bf16[128,2048]{1,0:T(8,128)(2,1)}, bf16[128,2048]{1,0:T(8,128)(2,1)}, f32[3,192,1024]{2,1,0:T(8,128)}) custom-call(bf16[128,2048]{1,0:T(8,128)(2,1)} %tok.1, bf16[128,2048]{1,0:T(8,128)(2,1)} %cot.1, s32[128,8]{1,0:T(8,128)} %copy.10.ids, f32[128,8]{1,0:T(8,128)} %copy.11.rw, bf16[384,320]{1,0:T(8,128)(2,1)} %constant.4.clone.perm, ...), custom_call_target="tpu_custom_call" | custom-call | tf_op jit(solution)/shard_map/expert_block/pallas_call | solution.py:323
  31.8 1.9 %copy.15 = bf16[128,2048]{1,0:T(8,128)(2,1)} copy(bf16[128,2048]{1,0:T(8,128)(2,1)} %get-tuple-element.6) | data formatting | bytes 1048576
  33.7 1.9 %copy.16 = bf16[128,2048]{1,0:T(8,128)(2,1)} copy(bf16[128,2048]{1,0:T(8,128)(2,1)} %get-tuple-element.7) | data formatting | bytes 1048576
  35.6 3.4 %copy.17 = f32[3,192,1024]{2,1,0:T(8,128)} copy(f32[3,192,1024]{2,1,0:T(8,128)} %get-tuple-element.8) | data formatting | bytes 4718592

commit v2 on v1

v2 whole, which is shorter than its diff:
```python
import functools

import jax
import jax.numpy as jnp
import numpy as np
from jax import lax
from jax.experimental import pallas as pl
from jax.experimental.pallas import tpu as pltpu
from jax.sharding import PartitionSpec as P

CAP = 10
PARTS = 4
VMEM_LIMIT = 61 * 1024 * 1024
MESH = pl.DeviceIdType.MESH
F32 = jnp.float32
BF16 = jnp.bfloat16


def round_up(value, unit):
    return -(-value // unit) * unit


class Sizes:
    def __init__(self, ep, edp, tp, tok_rows, feats, hid):
        self.ep, self.edp, self.tp = ep, edp, tp
        self.window = ep // PARTS
        self.tok_rows, self.feats, self.hid = tok_rows, feats, hid
        self.block = feats * tp // edp
        self.nblk = feats // self.block
        self.nch = max(1, min(4, self.block // 128))
        self.cw = self.block // self.nch
        self.xr = round_up(2 * CAP * self.nch, 16)
        self.rows = round_up(ep * CAP, 16)
        self.lanes = round_up(3 * ep * CAP, 128)


def permutations(z):
    table = np.zeros((z.nch, 2, z.rows, z.ep, z.xr), np.float32)
    factor = np.zeros((z.nch, z.lanes, z.ep, z.xr), np.float32)
    place = np.zeros((3, z.rows, z.lanes), np.float32)
    for i in range(z.ep):
        for c in range(CAP):
            for q in range(z.nch):
                for a in range(2):
                    table[q, a, i * CAP + c, i, (2 * q + a) * CAP + c] = 1.0
                for m in range(3):
                    factor[q, (m * z.ep + i) * CAP + c, i, (2 * q + m // 2) * CAP + c] = 1.0
            for m in range(3):
                place[m, i * CAP + c, (m * z.ep + i) * CAP + c] = 1.0
    flat = table.reshape(z.nch, 2 * z.rows, z.ep * z.xr)
    return (
        flat.reshape(-1, z.ep * z.xr), np.swapaxes(flat, 1, 2).copy(),
        factor.reshape(-1, z.ep * z.xr), place,
    )


def slot_parts(index, nch):
    chunk = jnp.zeros_like(index)
    for k in range(1, nch):
        chunk += (index >= 2 * CAP * k).astype(jnp.int32)
    rest = index - 2 * CAP * chunk
    array = (rest >= CAP).astype(jnp.int32)
    return chunk, array, rest - CAP * array


def kernel(
    z, tok_in, cot_in, ids_in, rw_in, perm_in, perm_t_in, factor_in, place_in, weights,
    left, right, summed, homes,
    tok, cot, ids, rw, perm, perm_t, factor, place,
    wb, x, xin, rb, rows, pout, pin, hb, lout, lb, ob, y, yin,
    in_sem, w_loc, w_send, w_recv, x_send, x_recv, r_send, r_recv, p_send, p_recv,
    l_send, l_recv, y_send, y_recv, q_send, q_recv,
):
    i, e, s = lax.axis_index("ep"), lax.axis_index("edp"), lax.axis_index("tp")
    barrier = pltpu.get_barrier_semaphore()
    group = z.ep * z.edp

    loads = [
        pltpu.make_async_copy(source, target, in_sem.at[k])
        for k, (source, target) in enumerate((
            (ids_in, ids), (rw_in, rw), (tok_in, tok), (cot_in, cot),
            (perm_in, perm), (perm_t_in, perm_t), (factor_in, factor), (place_in, place),
        ))
    ]
    for copy in loads[:4]:
        copy.start()

    def greet(step, carry):
        di = step // z.edp
        de = step - di * z.edp
        pl.semaphore_signal(
            barrier, inc=1,
            device_id=(lax.rem(i + di, z.ep), lax.rem(e + de, z.edp), s),
            device_id_type=MESH,
        )
        return carry

    for d in range(1, z.tp):
        pl.semaphore_signal(
            barrier, inc=1, device_id=(i, e, lax.rem(s + d, z.tp)), device_id_type=MESH
        )
    lax.fori_loop(1, group, greet, 0)

    own_w = pltpu.make_async_copy(
        weights.at[:, :, pl.ds(pl.multiple_of(s * z.feats, 128), z.feats)], wb.at[s], w_loc
    )
    own_w.start()
    for copy in loads[4:]:
        copy.start()

    row = lax.broadcasted_iota(jnp.int32, (z.xr, z.tok_rows), 0)
    chunk, array, slot = slot_parts(row, z.nch)
    in_use = row < 2 * CAP * z.nch
    before = (
        lax.broadcasted_iota(jnp.int32, (z.tok_rows, z.tok_rows), 0)
        < lax.broadcasted_iota(jnp.int32, (z.tok_rows, z.tok_rows), 1)
    ).astype(F32).astype(BF16)
    lane = lax.broadcasted_iota(jnp.int32, (z.tok_rows, z.xr), 1)
    lane_chunk, lane_array, _ = slot_parts(lane, z.nch)
    loads[0].wait()
    loads[1].wait()
    ids_t = ids[...]
    rw_t = rw[...]
    chosen, scales, picks = [], [], []
    for w in range(z.window):
        hit = (ids_t == w).astype(F32)
        match = jnp.sum(hit, axis=0, keepdims=True)
        weight = jnp.sum(hit * rw_t, axis=0, keepdims=True)
        match_all = jnp.broadcast_to(match, (z.xr, z.tok_rows))
        rank = jnp.dot(match_all.astype(BF16), before, preferred_element_type=F32)
        pick = jnp.where(in_use & (rank == slot.astype(F32)), match_all, 0.0)
        slot_weight = jnp.sum(pick * weight, axis=1, keepdims=True)
        picks.append(pick)
        scales.append((
            jnp.where(array[:, :1] == 1, slot_weight, 1.0), jnp.where(array[:, :1] == 0, slot_weight, 1.0),
        ))
        chosen.append([
            [jnp.where((chunk == q) & (array == a), pick, 0.0).astype(BF16) for a in range(2)]
            for q in range(z.nch)
        ])
    loads[2].wait()
    loads[3].wait()
    for b in range(z.nblk):
        for w in range(z.window):
            total = jnp.zeros((z.xr, z.cw), F32)
            for q in range(z.nch):
                cols = pl.ds(b * z.block + q * z.cw, z.cw)
                for a, source in ((0, tok), (1, cot)):
                    total += jnp.dot(chosen[w][q][a], source[:, cols], preferred_element_type=F32)
            x[w, b] = (total * scales[w][0]).astype(BF16)

    pl.semaphore_wait(barrier, group - 1 + z.tp - 1)

    sent = []
    for b in range(z.nblk):
        for d in range(1, z.ep):
            to = lax.rem(i + d, z.ep)
            sent.append(pltpu.make_async_remote_copy(
                src_ref=x.at[to // PARTS, b], dst_ref=xin.at[i, b],
                send_sem=x_send.at[d * z.nblk + b], recv_sem=x_recv.at[i * z.nblk + b],
                device_id=(to, e, s), device_id_type=MESH,
            ))
            sent[-1].start()
        for d in range(1, z.tp):
            to = lax.rem(s + d, z.tp)
            cols = pl.ds(pl.multiple_of(to * z.feats + b * z.block, 128), z.block)
            sent.append(pltpu.make_async_remote_copy(
                src_ref=weights.at[:, :, cols],
                dst_ref=wb.at[s, :, :, pl.ds(b * z.block, z.block)],
                send_sem=w_send.at[d * z.nblk + b], recv_sem=w_recv.at[s * z.nblk + b],
                device_id=(i, e, to), device_id_type=MESH,
            ))
            sent[-1].start()

    def right_copy(b, d):
        to = lax.rem(i + d, z.ep)
        return pltpu.make_async_remote_copy(
            src_ref=x.at[to // PARTS, b], dst_ref=rb.at[e, i],
            send_sem=r_send.at[b * z.ep + d], recv_sem=r_recv.at[0],
            device_id=(to, s * z.nblk + b, s), device_id_type=MESH,
        )

    for b in range(z.nblk):
        @pl.when(s * z.nblk + b != e)
        def _():
            for d in range(z.ep):
                right_copy(b, d).start()

    xin[i] = x[i // PARTS]
    for w in range(z.window):
        home = jnp.transpose(picks[w])
        for q in range(z.nch):
            for a in range(2):
                homes[w, 2 * q + a] = jnp.where(
                    (lane_chunk == q) & (lane_array == a), home, 0.0
                ).astype(BF16)
    own_w.wait()
    for copy in loads[4:]:
        copy.wait()

    last = (((1,), (1,)), ((), ()))
    for b in range(z.nblk):
        for d in range(1, z.ep):
            source = lax.rem(i + d, z.ep)
            landed = xin.at[source, b]
            pltpu.make_async_copy(landed, landed, x_recv.at[source * z.nblk + b]).wait()
        flat = jnp.dot(
            perm[...], xin[:, b].reshape(z.ep * z.xr, z.cw), preferred_element_type=F32
        ).astype(BF16)
        block = pl.ds(b * z.block, z.block)
        for q in range(z.nch):
            cols = pl.ds(b * z.block + q * z.cw, z.cw)
            rows[:, cols] = flat[q * 2 * z.rows:(q + 1) * 2 * z.rows]
        for d in range(1, z.tp):
            source = lax.rem(s + d, z.tp)
            landed = wb.at[source, :, :, block]
            pltpu.make_async_copy(landed, landed, w_recv.at[source * z.nblk + b]).wait()
        for m in range(3):
            part = rows[:z.rows, block] if m < 2 else rows[z.rows:, block]
            for t in range(z.tp):
                value = lax.dot_general(part, wb[t, m, :, block], last, preferred_element_type=F32)
                if b:
                    value += pout[m, t]
                pout[m, t] = value
            if b == z.nblk - 1:
                for d in range(1, z.tp):
                    sent.append(pltpu.make_async_remote_copy(
                        src_ref=pout.at[m], dst_ref=pin.at[s, m],
                        send_sem=p_send.at[d * 3 + m], recv_sem=p_recv.at[s * 3 + m],
                        device_id=(i, e, lax.rem(s + d, z.tp)), device_id_type=MESH,
                    ))
                    sent[-1].start()
    for d in range(1, z.tp):
        source = lax.rem(s + d, z.tp)
        for m in range(3):
            landed = pin.at[source, m]
            pltpu.make_async_copy(landed, landed, p_recv.at[source * 3 + m]).wait()

    for t in range(z.tp):
        sums = []
        for m in range(3):
            value = pout[m, t]
            for d in range(1, z.tp):
                value += pin[lax.rem(s + d, z.tp), m, t]
            sums.append(value)
        gate, up, d_hidden = sums
        sig = jax.nn.sigmoid(gate)
        active = gate * sig
        hb[t, 0] = (d_hidden * up * sig * (1.0 + gate * (1.0 - sig))).astype(BF16)
        hb[t, 1] = (d_hidden * active).astype(BF16)
        hb[t, 2] = (active * up).astype(BF16)

    first = (((0,), (0,)), ((), ()))
    packed = jnp.zeros((z.hid, z.lanes), F32)
    for m in range(3):
        packed += lax.dot_general(hb[s, m], place[m], first, preferred_element_type=F32)
    lout[...] = packed.astype(BF16)
    for d in range(1, z.edp):
        sent.append(pltpu.make_async_remote_copy(
            src_ref=lout, dst_ref=lb.at[e], send_sem=l_send.at[d], recv_sem=l_recv.at[e],
            device_id=(i, lax.rem(e + d, z.edp), s), device_id_type=MESH,
        ))
        sent[-1].start()
    left[e] = lout[...]

    for b in range(z.nblk):
        block = pl.ds(b * z.block, z.block)
        out = jnp.zeros((z.rows, z.block), F32)
        back = jnp.zeros((z.rows, z.block), F32)
        for t in range(z.tp):
            out += jnp.dot(hb[t, 2], wb[t, 2, :, block], preferred_element_type=F32)
            back += jnp.dot(hb[t, 0], wb[t, 0, :, block], preferred_element_type=F32)
            back += jnp.dot(hb[t, 1], wb[t, 1, :, block], preferred_element_type=F32)
        ob[:z.rows] = out.astype(BF16)
        ob[z.rows:] = back.astype(BF16)
        total = jnp.zeros((z.ep * z.xr, z.cw), F32)
        for q in range(z.nch):
            total += jnp.dot(perm_t[q], ob[:, q * z.cw:(q + 1) * z.cw], preferred_element_type=F32)
        y[:, b] = total.astype(BF16).reshape(z.ep, z.xr, z.cw)
        for d in range(1, z.ep):
            to = lax.rem(i + d, z.ep)
            sent.append(pltpu.make_async_remote_copy(
                src_ref=y.at[to, b], dst_ref=yin.at[i, b],
                send_sem=y_send.at[d * z.nblk + b], recv_sem=y_recv.at[i * z.nblk + b],
                device_id=(to, e, s), device_id_type=MESH,
            ))
            sent[-1].start()
    yin[i] = y[i]

    owner = e // z.nblk
    mine = e - owner * z.nblk

    def relay(d):
        return pltpu.make_async_remote_copy(
            src_ref=rb, dst_ref=rb, send_sem=q_send.at[d], recv_sem=q_recv.at[0],
            device_id=(i, e, lax.rem(s + d, z.tp)), device_id_type=MESH,
        )

    @pl.when(s == owner)
    def _():
        for source in range(z.ep):
            rb[e, source] = xin[source, mine]
        others = rb.at[pl.ds(0, z.edp - 1)]
        pltpu.make_async_copy(others, others, r_recv.at[0]).wait()
        for d in range(1, z.tp):
            relay(d).start()

    @pl.when(s != owner)
    def _():
        pltpu.make_async_copy(rb, rb, q_recv.at[0]).wait()

    for r in range(z.edp):
        flat = jnp.dot(
            factor[...], rb[r].reshape(z.ep * z.xr, z.cw), preferred_element_type=F32
        ).astype(BF16)
        for q in range(z.nch):
            right[pl.ds(r * z.lanes, z.lanes), pl.ds(q * z.cw, z.cw)] = flat[
                q * z.lanes:(q + 1) * z.lanes
            ]

    for b in range(z.nblk):
        for d in range(1, z.ep):
            source = lax.rem(i + d, z.ep)
            landed = yin.at[source, b]
            pltpu.make_async_copy(landed, landed, y_recv.at[source * z.nblk + b]).wait()
        for w in range(z.window):
            total = yin[w * PARTS, b].astype(F32)
            for h in range(1, PARTS):
                total += yin[w * PARTS + h, b].astype(F32)
            summed[w, b] = (total * scales[w][1]).astype(BF16)

    for d in range(1, z.edp):
        source = lax.rem(e + d, z.edp)
        landed = lb.at[source]
        pltpu.make_async_copy(landed, landed, l_recv.at[source]).wait()
        left[source] = lb[source]

    for copy in sent:
        copy.wait_send()
    for b in range(z.nblk):
        @pl.when(s * z.nblk + b != e)
        def _():
            for d in range(z.ep):
                right_copy(b, d).wait_send()

    @pl.when(s == owner)
    def _():
        for d in range(1, z.tp):
            relay(d).wait_send()


def finish(z, left, right, summed, homes, mixed, grad_tok, wgrad, wg, mix, grad, sem):
    factors = jnp.concatenate([left[r] for r in range(z.edp)], axis=1)
    lane = lax.broadcasted_iota(jnp.int32, (z.hid, z.lanes), 1)
    width = z.ep * CAP
    copies = []
    for m in range(3):
        keep = ((lane >= m * width) & (lane < (m + 1) * width)).astype(F32).astype(BF16)
        keep = jnp.concatenate([keep] * z.edp, axis=1)
        wg[m] = jnp.dot(factors * keep, right[...], preferred_element_type=F32)
        copies.append(pltpu.make_async_copy(wg.at[m], wgrad.at[m], sem.at[m]))
        copies[-1].start()
    for a, target in ((0, mix), (1, grad)):
        for q in range(z.nch):
            for b in range(z.nblk):
                value = jnp.zeros((z.tok_rows, z.cw), F32)
                for w in range(z.window):
                    value += jnp.dot(homes[w, 2 * q + a], summed[w, b], preferred_element_type=F32)
                target[:, b * z.block + q * z.cw:b * z.block + (q + 1) * z.cw] = value.astype(BF16)
        copies.append(pltpu.make_async_copy(target, (mixed, grad_tok)[a], sem.at[3 + a]))
        copies[-1].start()
    for copy in copies:
        copy.wait()


def shards(tokens, cotangent, expert_ids, route_weights, expert_weights):
    z = Sizes(
        lax.axis_size("ep"), lax.axis_size("edp"), lax.axis_size("tp"),
        tokens.shape[0], tokens.shape[1], expert_weights.shape[1],
    )
    tables = [jnp.asarray(table, BF16) for table in permutations(z)]
    operands = [tokens, cotangent, expert_ids.T, route_weights.T] + tables
    vmem = pl.BlockSpec(memory_space=pltpu.VMEM)
    hbm = pl.BlockSpec(memory_space=pltpu.HBM)
    dma = pltpu.SemaphoreType.DMA
    between = (
        jax.ShapeDtypeStruct((z.edp, z.hid, z.lanes), BF16),
        jax.ShapeDtypeStruct((z.edp * z.lanes, z.block), BF16),
        jax.ShapeDtypeStruct((z.window, z.nblk, z.xr, z.cw), BF16),
        jax.ShapeDtypeStruct((z.window, 2 * z.nch, z.tok_rows, z.xr), BF16),
    )
    passed = pl.pallas_call(
        functools.partial(kernel, z),
        out_shape=between,
        in_specs=[hbm] * (len(operands) + 1),
        out_specs=(vmem,) * 4,
        scratch_shapes=[pltpu.VMEM(o.shape, o.dtype) for o in operands] + [
            pltpu.VMEM((z.tp, 3, z.hid, z.feats), BF16),
            pltpu.VMEM((z.window, z.nblk, z.xr, z.cw), BF16),
            pltpu.VMEM((z.ep, z.nblk, z.xr, z.cw), BF16),
            pltpu.VMEM((z.edp, z.ep, z.xr, z.cw), BF16),
            pltpu.VMEM((2 * z.rows, z.feats), BF16),
            pltpu.VMEM((3, z.tp, z.rows, z.hid), F32),
            pltpu.VMEM((z.tp, 3, z.tp, z.rows, z.hid), F32),
            pltpu.VMEM((z.tp, 3, z.rows, z.hid), BF16),
            pltpu.VMEM((z.hid, z.lanes), BF16),
            pltpu.VMEM((z.edp, z.hid, z.lanes), BF16),
            pltpu.VMEM((2 * z.rows, z.block), BF16),
            pltpu.VMEM((z.ep, z.nblk, z.xr, z.cw), BF16),
            pltpu.VMEM((z.ep, z.nblk, z.xr, z.cw), BF16),
            dma((len(operands),)), dma, dma((z.tp * z.nblk,)), dma((z.tp * z.nblk,)),
            dma((z.ep * z.nblk,)), dma((z.ep * z.nblk,)),
            dma((z.nblk * z.ep,)), dma((1,)), dma((z.tp * 3,)), dma((z.tp * 3,)),
            dma((z.edp,)), dma((z.edp,)), dma((z.ep * z.nblk,)), dma((z.ep * z.nblk,)),
            dma((z.tp,)), dma((1,)),
        ],
        compiler_params=pltpu.CompilerParams(
            collective_id=0, has_side_effects=True, vmem_limit_bytes=VMEM_LIMIT
        ),
        name="expert_block",
    )(*operands, expert_weights)
    return pl.pallas_call(
        functools.partial(finish, z),
        out_shape=(
            jax.ShapeDtypeStruct(tokens.shape, BF16),
            jax.ShapeDtypeStruct(tokens.shape, BF16),
            jax.ShapeDtypeStruct((3, z.hid, z.block), F32),
        ),
        in_specs=[vmem] * 4,
        out_specs=(hbm,) * 3,
        scratch_shapes=[
            pltpu.VMEM((3, z.hid, z.block), F32),
            pltpu.VMEM(tokens.shape, BF16),
            pltpu.VMEM(tokens.shape, BF16),
            dma((5,)),
        ],
        compiler_params=pltpu.CompilerParams(vmem_limit_bytes=VMEM_LIMIT),
        name="finish",
    )(*passed)


def solution(mesh):
    placed = (
        P(("ep", "edp"), "tp"),
        P(("ep", "edp"), "tp"),
        P(("ep", "edp"), None),
        P(("ep", "edp"), None),
        P(None, ("ep", "tp"), None),
    )
    return jax.shard_map(
        shards,
        mesh=mesh,
        in_specs=placed,
        out_specs=(P(("ep", "edp"), "tp"), P(("ep", "edp"), "tp"), P(None, ("ep", "tp"), "edp")),
        check_vma=False,
    )
```

time: 39.3 us -> 29.3 us (0.75)
  local copies, waits for them, and re-layouts: 9.95 us -> 0 us
    unnamed x5 -> x0, local copies, waits for them, and re-layouts: 9.95 us -> none
    pallas_call x1 -> x2, Pallas kernels: 28.4 us -> 28.2 us  [the longest x1 24.7 us: shards(): pl.pallas_call(functools.partial(kernel, z), out_shape=between, in_specs=...]
where the time goes in v2:
time: 29.3 us; the launch traced here: 28.9 us
  Pallas kernels  28.2 us (96%)
  between operations  0.64 us (2%)
    pallas_call x1, Pallas kernels, shards(): pl.pallas_call(functools.partial(kernel, z), out_shape=between, in_specs=...  24.7 us
    pallas_call x1, Pallas kernels, shards(): pl.pallas_call(functools.partial(finish, z), out_shape=(jax.ShapeDtypeStr...  3.53 us

profile of v2, /device:TPU:0, one launch (start us, length us, event | category | flops | bytes accessed | tf_op | source)
XLA Modules:
  0.0 28.9 jit_solution(16230036854590587045)
XLA Ops:
  0.6 24.7 %expert_block.1 = (bf16[4,192,128]{2,1,0:T(8,128)(2,1)}, bf16[512,1024]{1,0:T(8,128)(2,1)}, bf16[1,2,80,256]{3,2,1,0:T(8,128)(2,1)}, bf16[1,8,128,80]{3,2,1,0:T(8,128)(2,1)}) custom-call(bf16[128,2048]{1,0:T(8,128)(2,1)} %tok_in.1, bf16[128,2048]{1,0:T(8,128)(2,1)} %cot_in.1, s32[8,128]{1,0:T(8,128)} %bitcast.2, f32[8,128]{1,0:T(8,128)} %bitcast.3, ...), custom_call_target="tpu_custom_call" | custom-call | tf_op jit(solution)/shard_map/expert_block/pallas_call | solution.py:392
  25.3 3.5 %finish.1 = (bf16[128,2048]{1,0:T(8,128)(2,1)}, bf16[128,2048]{1,0:T(8,128)(2,1)}, f32[3,192,1024]{2,1,0:T(8,128)}) custom-call(bf16[4,192,128]{2,1,0:T(8,128)(2,1)} %get-tuple-element.7.left, bf16[512,1024]{1,0:T(8,128)(2,1)} %get-tuple-element.8.right, bf16[1,2,80,256]{3,2,1,0:T(8,128)(2,1)} %get-tuple-element.9.summed, ...), custom_call_target="tpu_custom_call" | custom-call | tf_op jit(solution)/shard_map/finish/pallas_call | solution.py:422

commit v3 on v2

--- a/solution.py
+++ b/solution.py
@@ -65,10 +65,10 @@
 
 def kernel(
     z, tok_in, cot_in, ids_in, rw_in, perm_in, perm_t_in, factor_in, place_in, weights,
-    left, right, summed, homes,
+    left, right_out, summed_out, homes_out,
     tok, cot, ids, rw, perm, perm_t, factor, place,
-    wb, x, xin, rb, rows, pout, pin, hb, lout, lb, ob, y, yin,
-    in_sem, w_loc, w_send, w_recv, x_send, x_recv, r_send, r_recv, p_send, p_recv,
+    wb, x, xin, rb, rows, pout, pin, hb, lout, lb, ob, y, yin, right, summed, homes,
+    out_sem, in_sem, w_loc, w_send, w_recv, x_send, x_recv, r_send, r_recv, p_send, p_recv,
     l_send, l_recv, y_send, y_recv, q_send, q_recv,
 ):
     i, e, s = lax.axis_index("ep"), lax.axis_index("edp"), lax.axis_index("tp")
@@ -138,29 +138,10 @@
             [jnp.where((chunk == q) & (array == a), pick, 0.0).astype(BF16) for a in range(2)]
             for q in range(z.nch)
         ])
-    loads[2].wait()
-    loads[3].wait()
-    for b in range(z.nblk):
-        for w in range(z.window):
-            total = jnp.zeros((z.xr, z.cw), F32)
-            for q in range(z.nch):
-                cols = pl.ds(b * z.block + q * z.cw, z.cw)
-                for a, source in ((0, tok), (1, cot)):
-                    total += jnp.dot(chosen[w][q][a], source[:, cols], preferred_element_type=F32)
-            x[w, b] = (total * scales[w][0]).astype(BF16)
-
     pl.semaphore_wait(barrier, group - 1 + z.tp - 1)
 
     sent = []
     for b in range(z.nblk):
-        for d in range(1, z.ep):
-            to = lax.rem(i + d, z.ep)
-            sent.append(pltpu.make_async_remote_copy(
-                src_ref=x.at[to // PARTS, b], dst_ref=xin.at[i, b],
-                send_sem=x_send.at[d * z.nblk + b], recv_sem=x_recv.at[i * z.nblk + b],
-                device_id=(to, e, s), device_id_type=MESH,
-            ))
-            sent[-1].start()
         for d in range(1, z.tp):
             to = lax.rem(s + d, z.tp)
             cols = pl.ds(pl.multiple_of(to * z.feats + b * z.block, 128), z.block)
@@ -169,6 +150,24 @@
                 dst_ref=wb.at[s, :, :, pl.ds(b * z.block, z.block)],
                 send_sem=w_send.at[d * z.nblk + b], recv_sem=w_recv.at[s * z.nblk + b],
                 device_id=(i, e, to), device_id_type=MESH,
+            ))
+            sent[-1].start()
+    loads[2].wait()
+    loads[3].wait()
+    for b in range(z.nblk):
+        for w in range(z.window):
+            total = jnp.zeros((z.xr, z.cw), F32)
+            for q in range(z.nch):
+                cols = pl.ds(b * z.block + q * z.cw, z.cw)
+                for a, source in ((0, tok), (1, cot)):
+                    total += jnp.dot(chosen[w][q][a], source[:, cols], preferred_element_type=F32)
+            x[w, b] = (total * scales[w][0]).astype(BF16)
+        for d in range(1, z.ep):
+            to = lax.rem(i + d, z.ep)
+            sent.append(pltpu.make_async_remote_copy(
+                src_ref=x.at[to // PARTS, b], dst_ref=xin.at[i, b],
+                send_sem=x_send.at[d * z.nblk + b], recv_sem=x_recv.at[i * z.nblk + b],
+                device_id=(to, e, s), device_id_type=MESH,
             ))
             sent[-1].start()
 
@@ -261,7 +260,26 @@
             device_id=(i, lax.rem(e + d, z.edp), s), device_id_type=MESH,
         ))
         sent[-1].start()
-    left[e] = lout[...]
+    written = [pltpu.make_async_copy(lout, left.at[e], out_sem.at[0])]
+    written[-1].start()
+
+    owner = e // z.nblk
+    mine = e - owner * z.nblk
+
+    def relay(d):
+        return pltpu.make_async_remote_copy(
+            src_ref=rb, dst_ref=rb, send_sem=q_send.at[d], recv_sem=q_recv.at[0],
+            device_id=(i, e, lax.rem(s + d, z.tp)), device_id_type=MESH,
+        )
+
+    @pl.when(s == owner)
+    def _():
+        for source in range(z.ep):
+            rb[e, source] = xin[source, mine]
+        others = rb.at[pl.ds(0, z.edp - 1)]
+        pltpu.make_async_copy(others, others, r_recv.at[0]).wait()
+        for d in range(1, z.tp):
+            relay(d).start()
 
     for b in range(z.nblk):
         block = pl.ds(b * z.block, z.block)
@@ -287,24 +305,6 @@
             sent[-1].start()
     yin[i] = y[i]
 
-    owner = e // z.nblk
-    mine = e - owner * z.nblk
-
-    def relay(d):
-        return pltpu.make_async_remote_copy(
-            src_ref=rb, dst_ref=rb, send_sem=q_send.at[d], recv_sem=q_recv.at[0],
-            device_id=(i, e, lax.rem(s + d, z.tp)), device_id_type=MESH,
-        )
-
-    @pl.when(s == owner)
-    def _():
-        for source in range(z.ep):
-            rb[e, source] = xin[source, mine]
-        others = rb.at[pl.ds(0, z.edp - 1)]
-        pltpu.make_async_copy(others, others, r_recv.at[0]).wait()
-        for d in range(1, z.tp):
-            relay(d).start()
-
     @pl.when(s != owner)
     def _():
         pltpu.make_async_copy(rb, rb, q_recv.at[0]).wait()
@@ -317,6 +317,9 @@
             right[pl.ds(r * z.lanes, z.lanes), pl.ds(q * z.cw, z.cw)] = flat[
                 q * z.lanes:(q + 1) * z.lanes
             ]
+    for k, (source, target) in enumerate(((homes, homes_out), (right, right_out))):
+        written.append(pltpu.make_async_copy(source, target, out_sem.at[z.edp + k]))
+        written[-1].start()
 
     for b in range(z.nblk):
         for d in range(1, z.ep):
@@ -328,15 +331,20 @@
             for h in range(1, PARTS):
                 total += yin[w * PARTS + h, b].astype(F32)
             summed[w, b] = (total * scales[w][1]).astype(BF16)
+    written.append(pltpu.make_async_copy(summed, summed_out, out_sem.at[z.edp + 2]))
+    written[-1].start()
 
     for d in range(1, z.edp):
         source = lax.rem(e + d, z.edp)
         landed = lb.at[source]
         pltpu.make_async_copy(landed, landed, l_recv.at[source]).wait()
-        left[source] = lb[source]
+        written.append(pltpu.make_async_copy(landed, left.at[source], out_sem.at[d]))
+        written[-1].start()
 
     for copy in sent:
         copy.wait_send()
+    for copy in written:
+        copy.wait()
     for b in range(z.nblk):
         @pl.when(s * z.nblk + b != e)
         def _():
@@ -349,25 +357,43 @@
             relay(d).wait_send()
 
 
-def finish(z, left, right, summed, homes, mixed, grad_tok, wgrad, wg, mix, grad, sem):
-    factors = jnp.concatenate([left[r] for r in range(z.edp)], axis=1)
-    lane = lax.broadcasted_iota(jnp.int32, (z.hid, z.lanes), 1)
+def finish(
+    z, left_in, right_in, summed_in, homes_in, mixed, grad_tok, wgrad,
+    left, right, summed, homes, wg, mix, grad, in_sem, sem,
+):
+    loads = [
+        pltpu.make_async_copy(source, target, in_sem.at[k])
+        for k, (source, target) in enumerate(
+            ((summed_in, summed), (homes_in, homes), (left_in, left), (right_in, right))
+        )
+    ]
+    for copy in loads:
+        copy.start()
+    lane = lax.broadcasted_iota(jnp.int32, (1, z.lanes), 1)
     width = z.ep * CAP
+    keeps = [((lane >= m * width) & (lane < (m + 1) * width)).astype(F32).astype(BF16) for m in range(3)]
+    loads[0].wait()
+    loads[1].wait()
     copies = []
+    for b in range(z.nblk):
+        value = jnp.zeros((2 * z.nch * z.tok_rows, z.cw), F32)
+        for w in range(z.window):
+            home = homes[w].reshape(2 * z.nch * z.tok_rows, z.xr)
+            value += jnp.dot(home, summed[w, b], preferred_element_type=F32)
+        for q in range(z.nch):
+            cols = pl.ds(b * z.block + q * z.cw, z.cw)
+            for a, target in ((0, mix), (1, grad)):
+                at = (2 * q + a) * z.tok_rows
+                target[:, cols] = value[at:at + z.tok_rows].astype(BF16)
+    for a, target in ((0, mix), (1, grad)):
+        copies.append(pltpu.make_async_copy(target, (mixed, grad_tok)[a], sem.at[3 + a]))
+        copies[-1].start()
+    loads[2].wait()
+    loads[3].wait()
     for m in range(3):
-        keep = ((lane >= m * width) & (lane < (m + 1) * width)).astype(F32).astype(BF16)
-        keep = jnp.concatenate([keep] * z.edp, axis=1)
-        wg[m] = jnp.dot(factors * keep, right[...], preferred_element_type=F32)
+        factors = jnp.concatenate([left[r] * keeps[m] for r in range(z.edp)], axis=1)
+        wg[m] = jnp.dot(factors, right[...], preferred_element_type=F32)
         copies.append(pltpu.make_async_copy(wg.at[m], wgrad.at[m], sem.at[m]))
-        copies[-1].start()
-    for a, target in ((0, mix), (1, grad)):
-        for q in range(z.nch):
-            for b in range(z.nblk):
-                value = jnp.zeros((z.tok_rows, z.cw), F32)
-                for w in range(z.window):
-                    value += jnp.dot(homes[w, 2 * q + a], summed[w, b], preferred_element_type=F32)
-                target[:, b * z.block + q * z.cw:b * z.block + (q + 1) * z.cw] = value.astype(BF16)
-        copies.append(pltpu.make_async_copy(target, (mixed, grad_tok)[a], sem.at[3 + a]))
         copies[-1].start()
     for copy in copies:
         copy.wait()
@@ -380,7 +406,6 @@
     )
     tables = [jnp.asarray(table, BF16) for table in permutations(z)]
     operands = [tokens, cotangent, expert_ids.T, route_weights.T] + tables
-    vmem = pl.BlockSpec(memory_space=pltpu.VMEM)
     hbm = pl.BlockSpec(memory_space=pltpu.HBM)
     dma = pltpu.SemaphoreType.DMA
     between = (
@@ -393,7 +418,7 @@
         functools.partial(kernel, z),
         out_shape=between,
         in_specs=[hbm] * (len(operands) + 1),
-        out_specs=(vmem,) * 4,
+        out_specs=(hbm,) * 4,
         scratch_shapes=[pltpu.VMEM(o.shape, o.dtype) for o in operands] + [
             pltpu.VMEM((z.tp, 3, z.hid, z.feats), BF16),
             pltpu.VMEM((z.window, z.nblk, z.xr, z.cw), BF16),
@@ -408,7 +433,8 @@
             pltpu.VMEM((2 * z.rows, z.block), BF16),
             pltpu.VMEM((z.ep, z.nblk, z.xr, z.cw), BF16),
             pltpu.VMEM((z.ep, z.nblk, z.xr, z.cw), BF16),
-            dma((len(operands),)), dma, dma((z.tp * z.nblk,)), dma((z.tp * z.nblk,)),
+        ] + [pltpu.VMEM(o.shape, o.dtype) for o in between[1:]] + [
+            dma((z.edp + 3,)), dma((len(operands),)), dma, dma((z.tp * z.nblk,)), dma((z.tp * z.nblk,)),
             dma((z.ep * z.nblk,)), dma((z.ep * z.nblk,)),
             dma((z.nblk * z.ep,)), dma((1,)), dma((z.tp * 3,)), dma((z.tp * 3,)),
             dma((z.edp,)), dma((z.edp,)), dma((z.ep * z.nblk,)), dma((z.ep * z.nblk,)),
@@ -426,13 +452,13 @@
             jax.ShapeDtypeStruct(tokens.shape, BF16),
             jax.ShapeDtypeStruct((3, z.hid, z.block), F32),
         ),
-        in_specs=[vmem] * 4,
+        in_specs=[hbm] * 4,
         out_specs=(hbm,) * 3,
-        scratch_shapes=[
+        scratch_shapes=[pltpu.VMEM(o.shape, o.dtype) for o in between] + [
             pltpu.VMEM((3, z.hid, z.block), F32),
             pltpu.VMEM(tokens.shape, BF16),
             pltpu.VMEM(tokens.shape, BF16),
-            dma((5,)),
+            dma((4,)), dma((5,)),
         ],
         compiler_params=pltpu.CompilerParams(vmem_limit_bytes=VMEM_LIMIT),
         name="finish",

time: 29.3 us -> 28.1 us (0.959)
  Pallas kernels: 28.2 us -> 27.2 us
    pallas_call x1, Pallas kernels: 24.7 us -> 23.9 us  [shards(): pl.pallas_call(functools.partial(kernel, z), out_shape=between, in_specs=...]
where the time goes in v3:
time: 28.1 us; the launch traced here: 27.9 us
  Pallas kernels  27.2 us (97%)
  between operations  0.64 us (2%)
    pallas_call x1, Pallas kernels, shards(): pl.pallas_call(functools.partial(kernel, z), out_shape=between, in_specs=...  23.9 us
    pallas_call x1, Pallas kernels, shards(): pl.pallas_call(functools.partial(finish, z), out_shape=(jax.ShapeDtypeStr...  3.31 us

profile of v3, /device:TPU:0, one launch (start us, length us, event | category | flops | bytes accessed | tf_op | source)
XLA Modules:
  0.0 27.9 jit_solution(12943573475736737920)
XLA Ops:
  0.6 23.9 %expert_block.1 = (bf16[4,192,128]{2,1,0:T(8,128)(2,1)}, bf16[512,1024]{1,0:T(8,128)(2,1)}, bf16[1,2,80,256]{3,2,1,0:T(8,128)(2,1)}, bf16[1,8,128,80]{3,2,1,0:T(8,128)(2,1)}) custom-call(bf16[128,2048]{1,0:T(8,128)(2,1)} %tok_in.1, bf16[128,2048]{1,0:T(8,128)(2,1)} %cot_in.1, s32[8,128]{1,0:T(8,128)} %bitcast.2, f32[8,128]{1,0:T(8,128)} %bitcast.3, ...), custom_call_target="tpu_custom_call" | custom-call | tf_op jit(solution)/shard_map/expert_block/pallas_call | solution.py:417
  24.6 3.3 %finish.1 = (bf16[128,2048]{1,0:T(8,128)(2,1)}, bf16[128,2048]{1,0:T(8,128)(2,1)}, f32[3,192,1024]{2,1,0:T(8,128)}) custom-call(bf16[4,192,128]{2,1,0:T(8,128)(2,1)} %get-tuple-element.7.left_in, bf16[512,1024]{1,0:T(8,128)(2,1)} %get-tuple-element.8.right_in, bf16[1,2,80,256]{3,2,1,0:T(8,128)(2,1)} %get-tuple-element.9.summed_in, ...), custom_call_target="tpu_custom_call" | custom-call | tf_op jit(solution)/shard_map/finish/pallas_call | solution.py:448
